TPU v7x, 32 devices: a whole 2x2x4 slice. The times are simulated.
32 devices in a mesh: ctx: 16 (over z, y, core), head: 2 (over x).
Axes of the slice: x: 2, y: 2, z: 4, core: 2. Of those that a mesh axis runs over, the one named last changes fastest.
Arguments:
- patch_hidden: bfloat16 [1024, 4096], P('ctx', 'head'), may hold values from -6 to 6
- queries: bfloat16 [1024, 32, 128], P('ctx', 'head'), may hold values from -6 to 6
- new_keys: bfloat16 [1024, 32, 128], P('ctx', 'head'), may hold values from -6 to 6
- new_values: bfloat16 [1024, 32, 128], P('ctx', 'head'), may hold values from -6 to 6
- cache_keys: bfloat16 [16384, 32, 128], P('ctx', 'head'), may hold values from -6 to 6
- cache_values: bfloat16 [16384, 32, 128], P('ctx', 'head'), may hold values from -6 to 6
- cache_request: int32 [16384], P('ctx'), may hold values from 0 to 7, never falling along the last dimension, each value on 1 to 4096 neighbouring positions
- new_request: int32 [1024], replicated, may hold values from 0 to 7, as said below
- out_weight: bfloat16 [32, 128, 4096], P('head'), may hold values from -0.375 to 0.375
- norm_gain: float32 [4096], replicated, may hold values from 0.1 to 1.9
- dec_kv_weight: bfloat16 [4096, 2, 1024], P(None, None, 'head'), may hold values from -0.09375 to 0.09375
- dec_query_weight: bfloat16 [1024, 1024], P(None, 'head'), may hold values from -0.1875 to 0.1875
- query_gain: float32 [64], replicated, may hold values from 0.1 to 1.9
- key_gain: float32 [64], replicated, may hold values from 0.1 to 1.9
- dec_out_weight: bfloat16 [1024, 1024], P('head'), may hold values from -0.75 to 0.75
- byte_states: bfloat16 [4096, 1024], P('ctx'), may hold values from -6 to 6
- byte_patch: int32 [4096], P('ctx'), may hold values from 0 to 1023, never falling along the last dimension, each value on 1 to 8 neighbouring positions
Outputs:
- patch_out: bfloat16 [1024, 4096], P('ctx', 'head')
- byte_out: bfloat16 [4096, 1024], P('ctx', 'head')
Inputs may be any that keep to these rules, and one draw needn't show every extreme that they name: `new_request`: never falls along the patches; every request of 0 to 7 has an even number, two or more, of new patches. `cache_request`: never falls along the cached patches; every request has one or more cached patches. `byte_patch`: never falls along the bytes; every new patch owns one or more bytes.
All inputs are finite; a program needn't handle non-finite values.
Results may differ from a plain program's by a relative error of at most 0.017.
Values may be sent and summed in bfloat16 or wider, within the bound.
No kernel may reach another device: no remote copies, remote signals or barrier semaphores. Data moves between devices by JAX's collectives and lax.ppermute only.
A program may use at most 128 MiB of HBM per device.

v0:
```python
import jax
import jax.numpy as jnp
from jax import lax
from jax.sharding import PartitionSpec as P

DEC_DH = 64


def row_norm(values, gain_values, epsilon):
    meansq = jnp.mean(values * values, axis=-1, keepdims=True)
    return values * lax.rsqrt(meansq + epsilon) * gain_values


def per_device(
    patch_hidden,
    queries,
    new_keys,
    new_values,
    cache_keys,
    cache_values,
    cache_request,
    new_request,
    out_weight,
    norm_gain,
    dec_kv_weight,
    dec_query_weight,
    query_gain,
    key_gain,
    dec_out_weight,
    byte_states,
    byte_patch,
):
    new_rows, local_heads, head_size = queries.shape
    cache_rows = cache_keys.shape[0]
    total_rows = new_request.shape[0]
    ctx_index = lax.axis_index("ctx")
    head_index = lax.axis_index("head")
    first_new = ctx_index * new_rows
    all_keys = jnp.transpose(jnp.concatenate([cache_keys, new_keys], 0), (1, 0, 2))
    all_values = jnp.transpose(jnp.concatenate([cache_values, new_values], 0), (1, 0, 2))
    own_request = lax.dynamic_slice_in_dim(new_request, first_new, new_rows)
    local_request = jnp.concatenate([cache_request, own_request])
    local_position = jnp.concatenate(
        [jnp.full((cache_rows,), -1, jnp.int32), first_new + jnp.arange(new_rows, dtype=jnp.int32)]
    )
    score_scale = head_size ** (-0.5)
    portion = lax.all_gather(queries, "ctx", axis=0, tiled=True)
    row_count = portion.shape[0]
    piece_index = jnp.arange(row_count, dtype=jnp.int32)
    visible = (local_request[None, :] == new_request[:, None]) & (
        local_position[None, :] <= piece_index[:, None]
    )

    def one_head(inputs):
        query_head, key_head, value_head = inputs
        scores = (
            jnp.einsum("qd,kd->qk", query_head, key_head, preferred_element_type=jnp.float32)
            * score_scale
        )
        highest = jnp.max(jnp.where(visible, scores, -1e30), axis=1)
        weights = jnp.where(visible, jnp.exp(scores - highest[:, None]), 0.0)
        mixed_rows = jnp.dot(
            weights.astype(jnp.bfloat16), value_head, preferred_element_type=jnp.float32
        )
        return (mixed_rows, jnp.sum(weights, axis=1), highest)

    pieces = lax.map(one_head, (jnp.transpose(portion, (1, 0, 2)), all_keys, all_values))
    partial_out, partial_total, partial_max = tuple((part_values for part_values in pieces))
    highest = lax.pmax(partial_max, "ctx")
    factor = jnp.exp(partial_max - highest)
    summed_out, summed_total = (
        lax.psum_scatter(partial_out * factor[..., None], "ctx", scatter_dimension=1, tiled=True),
        lax.psum_scatter(partial_total * factor, "ctx", scatter_dimension=1, tiled=True),
    )
    attended = (summed_out / summed_total[..., None]).astype(jnp.bfloat16)
    flattened = jnp.transpose(attended, (1, 0, 2)).reshape(new_rows, local_heads * head_size)
    head_terms = jnp.dot(
        flattened,
        out_weight.reshape(local_heads * head_size, -1),
        preferred_element_type=jnp.float32,
    )
    model_width = head_terms.shape[1]
    slice_width = patch_hidden.shape[1]
    projected = lax.psum_scatter(head_terms, "head", scatter_dimension=1, tiled=True)
    patch_out = (patch_hidden.astype(jnp.float32) + projected).astype(jnp.bfloat16)
    widened = patch_out.astype(jnp.float32)
    squares = lax.psum(jnp.sum(widened * widened, axis=1), "head")
    gain_part = lax.dynamic_slice_in_dim(norm_gain, head_index * slice_width, slice_width)
    normed_part = (widened * lax.rsqrt(squares / model_width + 1e-05)[:, None] * gain_part).astype(
        jnp.bfloat16
    )
    normed = lax.all_gather(normed_part, "head", axis=1, tiled=True)
    dec_width = dec_kv_weight.shape[2]
    dec_heads = dec_width // DEC_DH
    patch_proj = jnp.dot(
        normed,
        dec_kv_weight.reshape(dec_kv_weight.shape[0], 2 * dec_width),
        preferred_element_type=jnp.float32,
    )
    patch_keys = row_norm(
        patch_proj[:, :dec_width].reshape(new_rows, dec_heads, DEC_DH), key_gain, 1e-06
    ).astype(jnp.bfloat16)
    patch_values = (
        patch_proj[:, dec_width:].astype(jnp.bfloat16).reshape(new_rows, dec_heads, DEC_DH)
    )
    byte_rows = byte_states.shape[0]
    query_proj = jnp.dot(byte_states, dec_query_weight, preferred_element_type=jnp.float32).reshape(
        byte_rows, dec_heads, DEC_DH
    )
    byte_query = row_norm(query_proj, query_gain, 1e-06).astype(jnp.bfloat16)
    table_index = jnp.arange(total_rows, dtype=jnp.int32)
    owner_table = table_index[None, :] == byte_patch[:, None]
    byte_request = jnp.sum(jnp.where(owner_table, new_request[None, :], 0), axis=1)
    dec_scale = DEC_DH ** (-0.5)
    piece_keys = lax.all_gather(patch_keys, "ctx", axis=0, tiled=True)
    piece_values = lax.all_gather(patch_values, "ctx", axis=0, tiled=True)
    row_count = piece_keys.shape[0]
    patch_index = jnp.arange(row_count, dtype=jnp.int32)
    fold_visible = (new_request[None, :] == byte_request[:, None]) & (
        patch_index[None, :] <= byte_patch[:, None]
    )
    scores = (
        jnp.einsum("bhd,jhd->hbj", byte_query, piece_keys, preferred_element_type=jnp.float32)
        * dec_scale
    )
    weights = jnp.where(fold_visible[None], jnp.exp(scores), 0.0)
    mixed_rows = jnp.einsum(
        "hbj,jhd->bhd",
        weights.astype(jnp.bfloat16),
        piece_values,
        preferred_element_type=jnp.float32,
    )
    denominator = jnp.transpose(jnp.sum(weights, axis=2))
    byte_mixed = (
        (mixed_rows / denominator[..., None]).astype(jnp.bfloat16).reshape(byte_rows, dec_width)
    )
    byte_terms = jnp.dot(byte_mixed, dec_out_weight, preferred_element_type=jnp.float32)
    byte_sum = lax.psum_scatter(byte_terms, "head", scatter_dimension=1, tiled=True)
    out_width = byte_sum.shape[1]
    own_states = lax.dynamic_slice_in_dim(byte_states, head_index * out_width, out_width, 1)
    byte_out = (own_states.astype(jnp.float32) + byte_sum).astype(jnp.bfloat16)
    return (patch_out, byte_out)


def solution(mesh):
    placed = (
        P("ctx", "head"),
        P("ctx", "head", None),
        P("ctx", "head", None),
        P("ctx", "head", None),
        P("ctx", "head", None),
        P("ctx", "head", None),
        P("ctx"),
        P(),
        P("head", None, None),
        P(),
        P(None, None, "head"),
        P(None, "head"),
        P(),
        P(),
        P("head", None),
        P("ctx", None),
        P("ctx"),
    )
    return jax.shard_map(
        per_device,
        mesh=mesh,
        in_specs=placed,
        out_specs=(P("ctx", "head"), P("ctx", "head")),
        check_vma=False,
    )
```

profile of v0, /device:TPU:0, one launch (start us, length us, event | category | flops | bytes accessed | tf_op | source)
XLA Modules:
  0.0 629.6 jit_solution(7363839396870362774)
XLA Ops:
  7.2 1.8 copy.44
  9.2 5.4 copy.45
  14.6 3.1 copy.47
  18.0 6.0 maximum_bitcast_fusion
  24.0 39.9 %all-gather.4.cloned.1.call-done = bf16[1024,16,128]{2,0,1:T(8,128)(2,1)} async-done(((bf16[64,16,128]{2,0,1:T(8,128)(2,1)}), bf16[1024,16,128]{2,0,1:T(8,128)(2,1)}) %all-gather.4.cloned.1.call-update) | async-done | bytes 4194320 | tf_op jit(solution)/shard_map/all_gather | solution.py:47
  63.9 143.5 %while.15 = (s32[]{:T(128)}, f32[16,1024,128]{2,1,0:T(8,128)}, f32[16,1024]{1,0:T(8,128)S(1)}, f32[16,1024]{1,0:T(8,128)}, bf16[16,1024,128]{2,1,0:T(8,128)(2,1)...) while((s32[]{:T(128)}, f32[16,1024,128]{2,1,0:T(8,128)}, ...), condition=%wide.region_3.4_spmd.clone, body=%wide.region_0.3_spmd.clone.sunk | while | flops 590477312 | bytes 14786173 | solution.py:67
  63.9 2.5 select_reduce_fusion.3
  66.4 3.4 fusion.74
  69.8 1.5 fusion.75
  72.9 2.5 select_reduce_fusion.3
  75.4 3.4 fusion.74
  78.7 1.5 fusion.75
  81.8 2.5 select_reduce_fusion.3
  84.3 3.4 fusion.74
  87.7 1.5 fusion.75
  90.8 2.5 select_reduce_fusion.3
  93.3 3.4 fusion.74
  96.7 1.5 fusion.75
  99.7 2.5 select_reduce_fusion.3
  102.2 3.4 fusion.74
  105.6 1.5 fusion.75
  108.7 2.5 select_reduce_fusion.3
  111.2 3.4 fusion.74
  114.6 1.5 fusion.75
  117.7 2.5 select_reduce_fusion.3
  120.2 3.4 fusion.74
  123.6 1.5 fusion.75
  126.7 2.5 select_reduce_fusion.3
  129.1 3.4 fusion.74
  132.5 1.5 fusion.75
  135.6 2.5 select_reduce_fusion.3
  138.1 3.4 fusion.74
  144.6 2.5 select_reduce_fusion.3
  147.1 3.4 fusion.74
  150.5 1.5 fusion.75
  153.5 2.5 select_reduce_fusion.3
  156.0 3.4 fusion.74
  159.4 1.5 fusion.75
  162.5 2.5 select_reduce_fusion.3
  165.0 3.4 fusion.74
  171.5 2.5 select_reduce_fusion.3
  174.0 3.4 fusion.74
  180.4 2.5 select_reduce_fusion.3
  182.9 3.4 fusion.74
  189.4 2.5 select_reduce_fusion.3
  191.9 3.4 fusion.74
  198.4 2.5 select_reduce_fusion.3
  200.9 3.4 fusion.74
  207.4 84.9 %all-reduce.3.cloned.1.call-done = f32[16,1024]{1,0:T(8,128)} async-done(((f32[16,1024]{1,0:T(8,128)}), f32[16,1024]{1,0:T(8,128)}) %all-reduce.3.cloned.1.call-update) | async-done | bytes 65552 | tf_op jit(solution)/shard_map/pmax | solution.py:69
  294.3 7.9 %broadcast_multiply_fusion = f32[16,1024,128]{2,1,0:T(8,128)} fusion(f32[16,1024,128]{2,1,0:T(8,128)} %get-tuple-element.46, f32[16,1024]{1,0:T(8,128)S(1)} %get-tuple-element.97), kind=kLoop, calls=%fused_computation.29 | loop fusion | flops 2097152 | bytes 16842752 | tf_op jit(solution)/shard_map/mul | solution.py:72
  302.3 51.3 %reduce-scatter.13.cloned.1.call-done = f32[64,16]{1,0:T(8,128)} async-done(((f32[1024,16]{1,0:T(8,128)}), f32[64,16]{1,0:T(8,128)}) %reduce-scatter.13.cloned.1.call-update) | async-done | bytes 4112
  354.5 105.9 %reduce-scatter.7.cloned.1.call-done = f32[16,64,128]{2,1,0:T(8,128)} async-done(((f32[16,1024,128]{2,1,0:T(8,128)}), f32[16,64,128]{2,1,0:T(8,128)}) %reduce-scatter.7.cloned.1.call-update) | async-done | bytes 524304 | tf_op jit(solution)/shard_map/reduce_scatter | solution.py:72
  460.3 10.1 %convolution_bitcast_fusion = f32[64,4096]{1,0:T(8,128)} fusion(bf16[16,128,4096]{2,1,0:T(8,128)(2,1)} %param.27, f32[16,64,128]{2,1,0:T(8,128)} %reduce-scatter.7.cloned.1.call-done, f32[16,64]{1,0:T(8,128)S(1)} %copy.55), kind=kOutput, calls=%fused_computation.23 | convolution fusion | flops 1074003968 | bytes 18354176 | tf_op jit(solution)/shard_map/dot_general | solution.py:77
  470.7 9.4 %copy.56 = bf16[512,8,2,512]{3,1,2,0:T(8,128)(2,1)} copy(bf16[512,8,2,512]{3,2,1,0:T(2,128)(2,1)} %bitcast.64) | data formatting | bytes 16777216
  480.1 10.5 %reduce-scatter.9.cloned.1.call-done = f32[64,2048]{1,0:T(8,128)} async-done(((f32[64,4096]{1,0:T(8,128)}), f32[64,2048]{1,0:T(8,128)}) %reduce-scatter.9.cloned.1.call-update) | async-done | bytes 524304 | tf_op jit(solution)/shard_map/reduce_scatter | solution.py:84
  491.9 4.9 psum.7
  496.9 7.4 %all_gather.13 = bf16[64,4096]{1,0:T(8,128)(2,1)S(1)} all-gather(bf16[64,2048]{1,0:T(8,128)(2,1)S(1)} %fusion.48), channel_id=1, replica_groups=mesh['ctx'=16,'head'=2] {'head'}, dimensions={1}, use_global_device_ids=true | all-gather | bytes 786432 | tf_op jit(solution)/shard_map/all_gather | solution.py:92
  504.4 5.1 fusion.58
  512.8 39.5 %all-gather.8.cloned.1.call-done = bf16[1024,8,64]{2,0,1:T(8,128)(2,1)} async-done(((bf16[64,8,64]{2,0,1:T(8,128)(2,1)}), bf16[1024,8,64]{2,0,1:T(8,128)(2,1)}) %all-gather.8.cloned.1.call-update) | async-done | bytes 1048592 | tf_op jit(solution)/shard_map/all_gather | solution.py:115
  552.3 7.1 %fusion.22 = (f32[8,256]{1,0:T(8,128)S(1)}, f32[8,256,1024]{2,1,0:T(8,128)}) fusion(pred[256,1024]{1,0:T(8,128)(4,1)S(1)} %fusion.35, bf16[1024,8,64]{2,0,1:T(8,128)(2,1)} %all-gather.8.cloned.1.call-done, f32[256,8,64]{0,2,1:T(8,128)S(1)} %bitcast.66, f32[64]{0:T(128)S(1)} %copy-done.13, f32[256,8]{0,1:T(8,128)S(1)} %add_rsqrt_fusion), kind=kOutput, calls=%fused_computation.21 | convolution fusion | flops 275118080 | bytes 10240256 | tf_op jit(solution)/shard_map/bhd,jhd->hbj/dot_general | solution.py:123
  559.4 35.3 %all-gather.6.cloned.1.call-done = bf16[1024,8,64]{2,1,0:T(8,128)(2,1)} async-done(((bf16[64,8,64]{2,1,0:T(8,128)(2,1)}), bf16[1024,8,64]{2,1,0:T(8,128)(2,1)}) %all-gather.6.cloned.1.call-update) | async-done | bytes 1048592 | tf_op jit(solution)/shard_map/all_gather | solution.py:116
  594.7 5.5 fusion.41
  601.7 19.2 %reduce-scatter.11.cloned.1.call-done = f32[256,512]{1,0:T(8,128)} async-done(((f32[256,1024]{1,0:T(8,128)}), f32[256,512]{1,0:T(8,128)}) %reduce-scatter.11.cloned.1.call-update) | async-done | bytes 524304 | tf_op jit(solution)/shard_map/reduce_scatter | solution.py:138
  620.9 1.8 add_convert_fusion
  (111 shorter events, 43.0 us)
Async XLA Ops:
  7.2 593.1 %copy-start = (bf16[512,1024]{1,0:T(8,128)(2,1)S(1)}, bf16[512,1024]{1,0:T(8,128)(2,1)}, u32[]{:S(2)}) copy-start(bf16[512,1024]{1,0:T(8,128)(2,1)} %param.33) | copy-start | bytes 3145732
  7.2 56.7 %all-gather.4.cloned.1.call-start = ((), (), s32[]{:S(2)}) async-start(), calls=%async_computation.4 | async-start | bytes 4456448 | tf_op jit(solution)/shard_map/all_gather | solution.py:47
  9.1 283.3 %all-reduce.3.cloned.1.call-start = ((), (), s32[]{:S(2)}) async-start(), calls=%async_computation.5 | async-start | bytes 131072 | tf_op jit(solution)/shard_map/pmax | solution.py:69
  9.1 5.5 copy-start.1
  14.6 3.1 copy-start.5
  14.6 3.2 copy-start.6
  14.6 3.3 copy-start.8
  14.6 3.4 copy-start.10
  207.4 146.2 %reduce-scatter.13.cloned.1.call-start = ((), (), s32[]{:S(2)}) async-start(), calls=%async_computation.11 | async-start | bytes 557056
  294.3 166.0 %reduce-scatter.7.cloned.1.call-start = ((), (), s32[]{:S(2)}) async-start(), calls=%async_computation.6 | async-start | bytes 8912896 | tf_op jit(solution)/shard_map/reduce_scatter | solution.py:72
  302.3 188.3 %reduce-scatter.9.cloned.1.call-start = ((), (), s32[]{:S(2)}) async-start(), calls=%async_computation.7 | async-start | bytes 1572864 | tf_op jit(solution)/shard_map/reduce_scatter | solution.py:84
  470.4 81.8 %all-gather.8.cloned.1.call-start = ((), (), s32[]{:S(2)}) async-start(), calls=%async_computation.9 | async-start | bytes 2228224 | tf_op jit(solution)/shard_map/all_gather | solution.py:115
  470.7 9.4 %copy-start.11 = (f32[4096]{0:T(1024)S(1)}, f32[4096]{0:T(1024)}, u32[]{:S(2)}) copy-start(f32[4096]{0:T(1024)} %param.28) | copy-start | bytes 49156
  470.7 19.9 %copy-start.7 = (bf16[64,2048]{1,0:T(8,128)(2,1)S(1)}, bf16[64,2048]{1,0:T(8,128)(2,1)}, u32[]{:S(2)}) copy-start(bf16[64,2048]{1,0:T(8,128)(2,1)} %param.19) | copy-start | bytes 786436
  491.8 17.6 %copy-start.4 = (bf16[64,2048]{1,0:T(8,128)(2,1)}, bf16[64,2048]{1,0:T(8,128)(2,1)S(1)}, u32[]{:S(2)}) copy-start(bf16[64,2048]{1,0:T(8,128)(2,1)S(1)} %get-tuple-element.95) | copy-start | bytes 786436
  504.3 5.5 copy-start.12
  504.3 7.2 %copy-start.9 = (s32[256]{0:T(256)S(1)}, s32[256]{0:T(256)}, u32[]{:S(2)}) copy-start(s32[256]{0:T(256)} %param.35) | copy-start | bytes 3076
  504.3 7.5 %copy-start.2 = (bf16[256,1024]{1,0:T(8,128)(2,1)S(1)}, bf16[256,1024]{1,0:T(8,128)(2,1)}, u32[]{:S(2)}) copy-start(bf16[256,1024]{1,0:T(8,128)(2,1)} %param.34) | copy-start | bytes 1572868
  504.3 7.5 %copy-start.3 = (bf16[1024,512]{1,0:T(8,128)(2,1)S(1)}, bf16[1024,512]{1,0:T(8,128)(2,1)}, u32[]{:S(2)}) copy-start(bf16[1024,512]{1,0:T(8,128)(2,1)} %param.30) | copy-start | bytes 3145732
  504.3 47.9 %copy-start.13 = (f32[64]{0:T(128)S(1)}, f32[64]{0:T(128)}, u32[]{:S(2)}) copy-start(f32[64]{0:T(128)} %param.31) | copy-start | bytes 772
  510.6 84.0 %all-gather.6.cloned.1.call-start = ((), (), s32[]{:S(2)}) async-start(), calls=%async_computation.8 | async-start | bytes 2228224 | tf_op jit(solution)/shard_map/all_gather | solution.py:116
  511.5 109.4 %reduce-scatter.11.cloned.1.call-start = ((), (), s32[]{:S(2)}) async-start(), calls=%async_computation.10 | async-start | bytes 1572864 | tf_op jit(solution)/shard_map/reduce_scatter | solution.py:138
Sparse Core Ops, SparseCore 0:
  10.7 53.1 all-gather.3
  207.5 84.7 all-reduce.2
  295.9 57.6 reduce-scatter.12
  357.6 102.7 reduce-scatter.6
  470.6 20.0 reduce-scatter.8
  510.8 41.4 all-gather.7
  554.4 40.1 all-gather.5
  601.8 19.0 reduce-scatter.10
where the time goes:
time: 632 us; the launch traced here: 630 us
  waiting for transfers between devices  387 us (61%)
  matrix products  124 us (20%)
  local copies, waits for them, and re-layouts  46.9 us (7%)
  other arithmetic  44.4 us (7%)
  between operations  14.4 us (2%)
  blocking collectives  12.3 us (2%)
    reduce_scatter x1, waiting for transfers between devices, per_device(): lax.psum_scatter(partial_out * factor[..., None], 'ctx', scatter_dimensio...  106 us
    pmax x1, waiting for transfers between devices, per_device(): highest = lax.pmax(partial_max, 'ctx')  84.9 us
    dot_general x16, matrix products, one_head(): jnp.dot(weights.astype(jnp.bfloat16), value_head, preferred_element_type=...  54.4 us
    unnamed x9, waiting for transfers between devices  51.4 us
    all_gather x1, waiting for transfers between devices, per_device(): portion = lax.all_gather(queries, 'ctx', axis=0, tiled=True)  39.9 us
    dot_general x16, matrix products, one_head(): jnp.einsum('qd,kd->qk', query_head, key_head, preferred_element_type=jnp....  39.8 us
    all_gather x1, waiting for transfers between devices, per_device(): piece_keys = lax.all_gather(patch_keys, 'ctx', axis=0, tiled=True)  39.5 us
    all_gather x1, waiting for transfers between devices, per_device(): piece_values = lax.all_gather(patch_values, 'ctx', axis=0, tiled=True)  35.3 us
  transfers between devices with their start and end apart: 8, of which 8 were waited for; matrix products, arithmetic and copies ran while one was open for 7% of the time, Pallas kernels for 0%

commit v1 on v0

--- a/solution.py
+++ b/solution.py
@@ -112,8 +112,13 @@
     owner_table = table_index[None, :] == byte_patch[:, None]
     byte_request = jnp.sum(jnp.where(owner_table, new_request[None, :], 0), axis=1)
     dec_scale = DEC_DH ** (-0.5)
-    piece_keys = lax.all_gather(patch_keys, "ctx", axis=0, tiled=True)
-    piece_values = lax.all_gather(patch_values, "ctx", axis=0, tiled=True)
+    piece_keys, piece_values = jnp.split(
+        lax.all_gather(
+            jnp.concatenate([patch_keys, patch_values], axis=1), "ctx", axis=0, tiled=True
+        ),
+        [patch_keys.shape[1]],
+        axis=1,
+    )
     row_count = piece_keys.shape[0]
     patch_index = jnp.arange(row_count, dtype=jnp.int32)
     fold_visible = (new_request[None, :] == byte_request[:, None]) & (

time: 632 us -> 600 us (0.949)
  waiting for transfers between devices: 387 us -> 361 us
  matrix products: 124 us -> 116 us
    all_gather x2 -> x1, waiting for transfers between devices: 74.8 us -> 49.3 us  [per_device(): lax.all_gather(jnp.concatenate([patch_keys, patch_values], axis=1), 'ctx'...]
    unnamed x9 -> x8, waiting for transfers between devices: 51.4 us -> 51.4 us
  transfers between devices with their start and end apart: 8 -> 7, of which waited for: 8 -> 7; matrix products, arithmetic and copies ran while one was open for 7% -> 6% of each run, Pallas kernels for 0% -> 0%
where the time goes in v1:
time: 600 us; the launch traced here: 598 us
  waiting for transfers between devices  361 us (60%)
  matrix products  116 us (19%)
  local copies, waits for them, and re-layouts  48.9 us (8%)
  other arithmetic  44.5 us (7%)
  between operations  14.4 us (2%)
  blocking collectives  12.3 us (2%)
    reduce_scatter x1, waiting for transfers between devices, per_device(): lax.psum_scatter(partial_out * factor[..., None], 'ctx', scatter_dimensio...  106 us
    pmax x1, waiting for transfers between devices, per_device(): highest = lax.pmax(partial_max, 'ctx')  84.9 us
    dot_general x16, matrix products, one_head(): jnp.dot(weights.astype(jnp.bfloat16), value_head, preferred_element_type=...  54.4 us
    unnamed x8, waiting for transfers between devices  51.4 us
    all_gather x1, waiting for transfers between devices, per_device(): lax.all_gather(jnp.concatenate([patch_keys, patch_values], axis=1), 'ctx'...  49.3 us
    all_gather x1, waiting for transfers between devices, per_device(): portion = lax.all_gather(queries, 'ctx', axis=0, tiled=True)  39.9 us
    dot_general x16, matrix products, one_head(): jnp.einsum('qd,kd->qk', query_head, key_head, preferred_element_type=jnp....  39.8 us
    reduce_sum x16, other arithmetic, one_head(): return (mixed_rows, jnp.sum(weights, axis=1), highest)  24.7 us
  transfers between devices with their start and end apart: 7, of which 7 were waited for; matrix products, arithmetic and copies ran while one was open for 6% of the time, Pallas kernels for 0%

profile of v1, /device:TPU:0, one launch (start us, length us, event | category | flops | bytes accessed | tf_op | source)
XLA Modules:
  0.0 597.6 jit_solution(6871329275759768042)
XLA Ops:
  7.2 1.8 copy.43
  9.2 5.4 copy.44
  14.6 3.1 copy.46
  18.0 6.0 %maximum_bitcast_fusion = (bf16[16,1088,128]{2,1,0:T(8,128)(2,1)}, bf16[16,1088,128]{2,1,0:T(8,128)(2,1)}) fusion(bf16[64,16,128]{2,0,1:T(8,128)(2,1)S(1)} %copy.45, bf16[1024,16,128]{2,0,1:T(8,128)(2,1)} %copy.44, bf16[64,16,128]{2,0,1:T(8,128)(2,1)S(1)} %copy.47, bf16[1024,16,128]{2,0,1:T(8,128)(2,1)} %copy.46), kind=kLoop, calls=%fused_computation.24 | loop fusion | flops 17825792 | bytes 17825792 | tf_op jit(solution)/shard_map/transpose | solution.py:39
  24.0 39.9 %all-gather.3.cloned.1.call-done = bf16[1024,16,128]{2,0,1:T(8,128)(2,1)} async-done(((bf16[64,16,128]{2,0,1:T(8,128)(2,1)}), bf16[1024,16,128]{2,0,1:T(8,128)(2,1)}) %all-gather.3.cloned.1.call-update) | async-done | bytes 4194320 | tf_op jit(solution)/shard_map/all_gather | solution.py:47
  63.9 143.5 %while.15 = (s32[]{:T(128)}, f32[16,1024,128]{2,1,0:T(8,128)}, f32[16,1024]{1,0:T(8,128)S(1)}, f32[16,1024]{1,0:T(8,128)}, bf16[16,1024,128]{2,1,0:T(8,128)(2,1)...) while((s32[]{:T(128)}, f32[16,1024,128]{2,1,0:T(8,128)}, ...), condition=%wide.region_3.4_spmd.clone, body=%wide.region_0.3_spmd.clone.sunk | while | flops 590477312 | bytes 14786173 | solution.py:67
  63.9 2.5 select_reduce_fusion.3
  66.4 3.4 fusion.73
  69.8 1.5 fusion.74
  72.9 2.5 select_reduce_fusion.3
  75.4 3.4 fusion.73
  78.8 1.5 fusion.74
  81.8 2.5 select_reduce_fusion.3
  84.3 3.4 fusion.73
  87.7 1.5 fusion.74
  90.8 2.5 select_reduce_fusion.3
  93.3 3.4 fusion.73
  99.7 2.5 select_reduce_fusion.3
  102.2 3.4 fusion.73
  105.6 1.5 fusion.74
  108.7 2.5 select_reduce_fusion.3
  111.2 3.4 fusion.73
  114.6 1.5 fusion.74
  117.7 2.5 select_reduce_fusion.3
  120.2 3.4 fusion.73
  123.5 1.5 fusion.74
  126.6 2.5 select_reduce_fusion.3
  129.1 3.4 fusion.73
  132.5 1.5 fusion.74
  135.6 2.5 select_reduce_fusion.3
  138.1 3.4 fusion.73
  141.5 1.5 fusion.74
  144.6 2.5 select_reduce_fusion.3
  147.1 3.4 fusion.73
  153.5 2.5 select_reduce_fusion.3
  156.0 3.4 fusion.73
  159.4 1.5 fusion.74
  162.5 2.5 select_reduce_fusion.3
  165.0 3.4 fusion.73
  168.4 1.5 fusion.74
  171.5 2.5 select_reduce_fusion.3
  174.0 3.4 fusion.73
  180.5 2.5 select_reduce_fusion.3
  182.9 3.4 fusion.73
  189.4 2.5 select_reduce_fusion.3
  191.9 3.4 fusion.73
  198.4 2.5 select_reduce_fusion.3
  200.9 3.4 fusion.73
  207.4 84.9 %all-reduce.3.cloned.1.call-done = f32[16,1024]{1,0:T(8,128)} async-done(((f32[16,1024]{1,0:T(8,128)}), f32[16,1024]{1,0:T(8,128)}) %all-reduce.3.cloned.1.call-update) | async-done | bytes 65552 | tf_op jit(solution)/shard_map/pmax | solution.py:69
  294.3 7.9 %broadcast_multiply_fusion = f32[16,1024,128]{2,1,0:T(8,128)} fusion(f32[16,1024,128]{2,1,0:T(8,128)} %get-tuple-element.46, f32[16,1024]{1,0:T(8,128)S(1)} %get-tuple-element.97), kind=kLoop, calls=%fused_computation.29 | loop fusion | flops 2097152 | bytes 16842752 | tf_op jit(solution)/shard_map/mul | solution.py:72
  302.3 51.3 %reduce-scatter.13.cloned.1.call-done = f32[64,16]{1,0:T(8,128)} async-done(((f32[1024,16]{1,0:T(8,128)}), f32[64,16]{1,0:T(8,128)}) %reduce-scatter.13.cloned.1.call-update) | async-done | bytes 4112
  354.4 105.9 %reduce-scatter.7.cloned.1.call-done = f32[16,64,128]{2,1,0:T(8,128)} async-done(((f32[16,1024,128]{2,1,0:T(8,128)}), f32[16,64,128]{2,1,0:T(8,128)}) %reduce-scatter.7.cloned.1.call-update) | async-done | bytes 524304 | tf_op jit(solution)/shard_map/reduce_scatter | solution.py:72
  460.3 10.1 %convolution_bitcast_fusion = f32[64,4096]{1,0:T(8,128)} fusion(bf16[16,128,4096]{2,1,0:T(8,128)(2,1)} %param.27, f32[16,64,128]{2,1,0:T(8,128)} %reduce-scatter.7.cloned.1.call-done, f32[16,64]{1,0:T(8,128)S(1)} %copy.55), kind=kOutput, calls=%fused_computation.23 | convolution fusion | flops 1074003968 | bytes 18354176 | tf_op jit(solution)/shard_map/dot_general | solution.py:77
  470.7 9.4 %copy.58 = bf16[512,8,2,512]{3,1,2,0:T(8,128)(2,1)} copy(bf16[512,8,2,512]{3,2,1,0:T(2,128)(2,1)} %bitcast.63) | data formatting | bytes 16777216
  480.0 10.6 %reduce-scatter.9.cloned.1.call-done = f32[64,2048]{1,0:T(8,128)} async-done(((f32[64,4096]{1,0:T(8,128)}), f32[64,2048]{1,0:T(8,128)}) %reduce-scatter.9.cloned.1.call-update) | async-done | bytes 524304 | tf_op jit(solution)/shard_map/reduce_scatter | solution.py:84
  491.8 4.9 psum.7
  496.9 7.4 %all_gather.10 = bf16[64,4096]{1,0:T(8,128)(2,1)S(1)} all-gather(bf16[64,2048]{1,0:T(8,128)(2,1)S(1)} %fusion.50), channel_id=1, replica_groups=mesh['ctx'=16,'head'=2] {'head'}, dimensions={1}, use_global_device_ids=true | all-gather | bytes 786432 | tf_op jit(solution)/shard_map/all_gather | solution.py:92
  504.3 5.1 fusion.58
  512.2 49.3 %all-gather.5.cloned.1.call-done = bf16[1024,16,64]{2,1,0:T(8,128)(2,1)} async-done(((bf16[64,16,64]{2,1,0:T(8,128)(2,1)}), bf16[1024,16,64]{2,1,0:T(8,128)(2,1)}) %all-gather.5.cloned.1.call-update) | async-done | bytes 2097168 | tf_op jit(solution)/shard_map/all_gather | solution.py:116
  561.5 2.5 fusion.57
  564.0 2.7 fusion.22
  566.7 1.6 fusion.43
  569.8 19.1 %reduce-scatter.11.cloned.1.call-done = f32[256,512]{1,0:T(8,128)} async-done(((f32[256,1024]{1,0:T(8,128)}), f32[256,512]{1,0:T(8,128)}) %reduce-scatter.11.cloned.1.call-update) | async-done | bytes 524304 | tf_op jit(solution)/shard_map/reduce_scatter | solution.py:143
  588.9 1.8 add_convert_fusion
  (111 shorter events, 42.5 us)
Async XLA Ops:
  7.2 561.2 %copy-start = (bf16[512,1024]{1,0:T(8,128)(2,1)S(1)}, bf16[512,1024]{1,0:T(8,128)(2,1)}, u32[]{:S(2)}) copy-start(bf16[512,1024]{1,0:T(8,128)(2,1)} %param.33) | copy-start | bytes 3145732
  7.2 56.7 %all-gather.3.cloned.1.call-start = ((), (), s32[]{:S(2)}) async-start(), calls=%async_computation.4 | async-start | bytes 4456448 | tf_op jit(solution)/shard_map/all_gather | solution.py:47
  9.1 283.3 %all-reduce.3.cloned.1.call-start = ((), (), s32[]{:S(2)}) async-start(), calls=%async_computation.5 | async-start | bytes 131072 | tf_op jit(solution)/shard_map/pmax | solution.py:69
  9.1 5.5 copy-start.1
  14.6 3.1 copy-start.5
  14.6 3.2 copy-start.6
  14.6 3.3 copy-start.8
  14.6 3.4 copy-start.10
  207.4 146.2 %reduce-scatter.13.cloned.1.call-start = ((), (), s32[]{:S(2)}) async-start(), calls=%async_computation.10 | async-start | bytes 557056
  294.2 166.0 %reduce-scatter.7.cloned.1.call-start = ((), (), s32[]{:S(2)}) async-start(), calls=%async_computation.6 | async-start | bytes 8912896 | tf_op jit(solution)/shard_map/reduce_scatter | solution.py:72
  302.2 188.3 %reduce-scatter.9.cloned.1.call-start = ((), (), s32[]{:S(2)}) async-start(), calls=%async_computation.7 | async-start | bytes 1572864 | tf_op jit(solution)/shard_map/reduce_scatter | solution.py:84
  470.4 91.1 %all-gather.5.cloned.1.call-start = ((), (), s32[]{:S(2)}) async-start(), calls=%async_computation.8 | async-start | bytes 4456448 | tf_op jit(solution)/shard_map/all_gather | solution.py:116
  470.7 9.4 %copy-start.11 = (f32[4096]{0:T(1024)S(1)}, f32[4096]{0:T(1024)}, u32[]{:S(2)}) copy-start(f32[4096]{0:T(1024)} %param.28) | copy-start | bytes 49156
  470.7 19.9 %copy-start.7 = (bf16[64,2048]{1,0:T(8,128)(2,1)S(1)}, bf16[64,2048]{1,0:T(8,128)(2,1)}, u32[]{:S(2)}) copy-start(bf16[64,2048]{1,0:T(8,128)(2,1)} %param.19) | copy-start | bytes 786436
  491.8 17.6 %copy-start.4 = (bf16[64,2048]{1,0:T(8,128)(2,1)}, bf16[64,2048]{1,0:T(8,128)(2,1)S(1)}, u32[]{:S(2)}) copy-start(bf16[64,2048]{1,0:T(8,128)(2,1)S(1)} %get-tuple-element.95) | copy-start | bytes 786436
  504.3 5.7 copy-start.12
  504.3 6.7 %copy-start.9 = (s32[256]{0:T(256)S(1)}, s32[256]{0:T(256)}, u32[]{:S(2)}) copy-start(s32[256]{0:T(256)} %param.35) | copy-start | bytes 3076
  504.3 7.0 %copy-start.2 = (bf16[256,1024]{1,0:T(8,128)(2,1)S(1)}, bf16[256,1024]{1,0:T(8,128)(2,1)}, u32[]{:S(2)}) copy-start(bf16[256,1024]{1,0:T(8,128)(2,1)} %param.34) | copy-start | bytes 1572868
  504.3 7.0 %copy-start.3 = (bf16[1024,512]{1,0:T(8,128)(2,1)S(1)}, bf16[1024,512]{1,0:T(8,128)(2,1)}, u32[]{:S(2)}) copy-start(bf16[1024,512]{1,0:T(8,128)(2,1)} %param.30) | copy-start | bytes 3145732
  510.9 78.0 %reduce-scatter.11.cloned.1.call-start = ((), (), s32[]{:S(2)}) async-start(), calls=%async_computation.9 | async-start | bytes 1572864 | tf_op jit(solution)/shard_map/reduce_scatter | solution.py:143
  511.8 52.2 %copy-start.13 = (f32[64]{0:T(128)S(1)}, f32[64]{0:T(128)}, u32[]{:S(2)}) copy-start(f32[64]{0:T(128)} %param.31) | copy-start | bytes 772
Sparse Core Ops, SparseCore 0:
  10.7 53.1 all-gather.2
  207.5 84.7 all-reduce.2
  295.9 57.6 reduce-scatter.12
  357.5 102.7 reduce-scatter.6
  470.5 20.0 reduce-scatter.8
  511.1 50.3 all-gather.4
  569.9 18.9 reduce-scatter.10
